TPU v7x, 32 devices: a whole 2x2x4 slice. The times are simulated.
32 devices in a mesh: ctx: 8 (over z, core), tp: 4 (over y, x).
Axes of the slice: x: 2, y: 2, z: 4, core: 2. Of those that a mesh axis runs over, the one named last changes fastest.
Arguments:
- tokens: bfloat16 [2, 4096, 8192], P(None, 'ctx', 'tp'), may hold values from -14 to 14
- norm_gain: float32 [8192], replicated, may hold values from 0.5 to 1.5
- span_order: int32 [2, 16], replicated, may hold values from 0 to 15, each once within a row
- w_query: bfloat16 [8192, 4096], P('ctx', 'tp'), may hold values from -0.10122281 to 0.10122281
- w_key: bfloat16 [8192, 1024], P('ctx', 'tp'), may hold values from -0.10122281 to 0.10122281
- value_weight: bfloat16 [8192, 1024], P('ctx', 'tp'), may hold values from -0.0625 to 0.0625
- w_out: bfloat16 [4096, 8192], P('tp', 'ctx'), may hold values from -0.75 to 0.75
Outputs:
- mixed: bfloat16 [2, 4096, 8192], P(None, 'ctx', 'tp')
Inputs may be any that keep to these rules, and one draw needn't show every extreme that they name: Each row of span_order names every one of the 2 * 8 blocks of positions once; stored block b of a sequence holds positions span_order[b] * 256 onwards, in order.
All inputs are finite; a program needn't handle non-finite values.
Results may differ from a plain program's by a relative error of at most 0.014.
Values may be sent and summed in bfloat16 or wider, within the bound.
A program may use at most 128 MiB of HBM per device.

v0:
```python
import math
import jax
import jax.numpy as jnp
from jax import lax
from jax.sharding import PartitionSpec as P

HEAD_DIM = 128
theta_base = 500000.0
norm_eps = 1e-05
masked_score = -1e30


def normalize(flat_rows, norm_gain):
    wide = flat_rows.astype(jnp.float32)
    factor = lax.rsqrt(jnp.mean(wide * wide, axis=-1, keepdims=True) + norm_eps)
    return (wide * factor * norm_gain).astype(jnp.bfloat16)


def positions_of(span_order, first, count, block_rows):
    stored = first + jnp.arange(count, dtype=jnp.int32)
    which = stored // block_rows
    slots = jnp.arange(span_order.shape[1], dtype=jnp.int32)
    picked = jnp.sum(
        jnp.where(slots[None, None, :] == which[None, :, None], span_order[:, None, :], 0), axis=2
    )
    return picked * block_rows + stored % block_rows


def apply_rotation(value_rows, token_position, head_size):
    half = head_size // 2
    freqs = jnp.exp(-(2.0 * jnp.arange(half, dtype=jnp.float32) / head_size) * math.log(theta_base))
    angle = token_position.astype(jnp.float32)[..., None] * freqs
    cosine = jnp.cos(angle)[:, :, None, :]
    sine = jnp.sin(angle)[:, :, None, :]
    front = value_rows[..., :half]
    back = value_rows[..., half:]
    return jnp.concatenate([front * cosine - back * sine, back * cosine + front * sine], axis=-1)


def per_device(tokens, norm_gain, span_order, w_query, w_key, value_weight, w_out):
    sequence_batch, rows_dev, _ = tokens.shape
    head_size = HEAD_DIM
    query_heads = w_query.shape[1] // head_size
    key_heads = w_key.shape[1] // head_size
    group_width = query_heads // key_heads
    block_rows = rows_dev // 2
    total_rows = sequence_batch * rows_dev
    factor = 1.0 / math.sqrt(head_size)
    rank = lax.axis_index("ctx")
    whole = lax.all_gather(tokens, "tp", axis=2, tiled=True)
    normed = normalize(whole.reshape(total_rows, whole.shape[2]), norm_gain)
    query_pos = positions_of(span_order, rank * rows_dev, rows_dev, block_rows)
    latest = jnp.max(query_pos, axis=1)
    stat_shape = (sequence_batch, key_heads, group_width, rows_dev)
    initial = (
        jnp.full(stat_shape, masked_score, jnp.float32),
        jnp.zeros(stat_shape, jnp.float32),
        jnp.zeros(stat_shape + (head_size,), jnp.float32),
    )
    pieces = (
        lax.all_gather(w_query, "ctx", axis=0, tiled=True),
        lax.all_gather(w_key, "ctx", axis=0, tiled=True),
        lax.all_gather(value_weight, "ctx", axis=0, tiled=True),
    )
    query_flat, flattened_key, flattened_value = tuple(
        (jnp.dot(normed, piece, preferred_element_type=jnp.float32) for piece in pieces)
    )
    turned = apply_rotation(
        query_flat.reshape(sequence_batch, rows_dev, query_heads, head_size), query_pos, head_size
    ).astype(jnp.bfloat16)
    query = turned.reshape(sequence_batch, rows_dev, key_heads, group_width, head_size).transpose(
        0, 2, 3, 1, 4
    )
    turned = apply_rotation(
        flattened_key.reshape(sequence_batch, rows_dev, key_heads, head_size), query_pos, head_size
    ).astype(jnp.bfloat16)
    own_values = flattened_value.reshape(sequence_batch, rows_dev, key_heads, head_size).astype(
        jnp.bfloat16
    )
    key_piece = lax.all_gather(turned, "ctx", axis=1, tiled=True)
    value_piece = lax.all_gather(own_values, "ctx", axis=1, tiled=True)
    count = key_piece.shape[1]
    step_rows = 512

    def one_block(index, state):
        first = index * step_rows
        key_block = lax.dynamic_slice_in_dim(key_piece, first, step_rows, 1)
        value_block = lax.dynamic_slice_in_dim(value_piece, first, step_rows, 1)
        key_pos = positions_of(span_order, first, step_rows, block_rows)

        def update(current):
            peak, total, summed = current
            scores = (
                jnp.einsum(
                    "shgqd,skhd->shgqk", query, key_block, preferred_element_type=jnp.float32
                )
                * factor
            )
            allowed = key_pos[:, None, None, None, :] <= query_pos[:, None, None, :, None]
            scores = jnp.where(allowed, scores, masked_score)
            new_peak = jnp.maximum(peak, jnp.max(scores, axis=-1))
            weights = jnp.where(allowed, jnp.exp(scores - new_peak[..., None]), 0.0)
            shrink = jnp.exp(peak - new_peak)
            total = total * shrink + jnp.sum(weights, axis=-1)
            summed = summed * shrink[..., None] + jnp.einsum(
                "shgqk,skhd->shgqd",
                weights.astype(jnp.bfloat16),
                value_block,
                preferred_element_type=jnp.float32,
            )
            return (new_peak, total, summed)

        return lax.cond(
            jnp.all(jnp.min(key_pos, axis=1) > latest), lambda kept: kept, update, state
        )

    peak, total, summed = lax.fori_loop(0, count // step_rows, one_block, initial)
    attended = (summed / total[..., None]).astype(jnp.bfloat16)
    attended = attended.transpose(0, 3, 1, 2, 4).reshape(total_rows, query_heads * head_size)
    terms = jnp.dot(
        attended,
        lax.all_gather(w_out, "ctx", axis=1, tiled=True),
        preferred_element_type=jnp.float32,
    )
    mixed = lax.psum_scatter(terms.astype(jnp.bfloat16), "tp", scatter_dimension=1, tiled=True)
    return mixed.reshape(sequence_batch, rows_dev, mixed.shape[1])


def solution(mesh):
    placed = (
        P(None, "ctx", "tp"),
        P(),
        P(),
        P("ctx", "tp"),
        P("ctx", "tp"),
        P("ctx", "tp"),
        P("tp", "ctx"),
    )
    return jax.shard_map(
        per_device, mesh=mesh, in_specs=placed, out_specs=P(None, "ctx", "tp"), check_vma=False
    )
```

profile of v0, /device:TPU:0, one launch (start us, length us, event | category | flops | bytes accessed | tf_op | source)
XLA Modules:
  0.0 862.1 jit_solution(7252307660646929625)
XLA Ops:
  10.5 48.0 %all-gather.10.cloned.1.call-done = bf16[8192,256]{1,0:T(8,128)(2,1)} async-done(((bf16[1024,256]{1,0:T(8,128)(2,1)}), bf16[8192,256]{1,0:T(8,128)(2,1)}) %all-gather.10.cloned.1.call-update) | async-done | bytes 4194320 | tf_op jit(solution)/shard_map/all_gather | solution.py:62
  58.6 6.3 copy.24
  64.9 151.7 %all-gather.8.cloned.1.call-done = bf16[2,512,8192]{2,1,0:T(8,128)(2,1)} async-done(((bf16[2,512,2048]{2,1,0:T(8,128)(2,1)}), bf16[2,512,8192]{2,1,0:T(8,128)(2,1)}) %all-gather.8.cloned.1.call-update) | async-done | bytes 16777232 | tf_op jit(solution)/shard_map/all_gather | solution.py:50
  216.5 7.5 fusion.21
  224.0 9.0 %fusion.29 = f32[2,512,2,128]{1,3,2,0:T(8,128)S(1)} fusion(bf16[2,128,8192,1]{2,1,0,3:T(8,128)(2,1)S(1)} %bitcast.69, bf16[2,512,8192]{2,1,0:T(8,128)(2,1)} %all-gather.8.cloned.1.call-done, f32[8192]{0:T(1024)S(1)} %copy-done.2, f32[2,512]{1,0:T(2,128)S(1)} %add_rsqrt_fusion), kind=kOutput, calls=%fused_computation.49 | convolution fusion | flops 4328521728 | bytes 22056960 | tf_op jit(solution)/shard_map/dot_general | solution.py:66
  234.2 30.9 %all-gather.16.cloned.1.call-done = bf16[8192,256]{1,0:T(8,128)(2,1)} async-done(((bf16[1024,256]{1,0:T(8,128)(2,1)}), bf16[8192,256]{1,0:T(8,128)(2,1)}) %all-gather.16.cloned.1.call-update) | async-done | bytes 4194320 | tf_op jit(solution)/shard_map/all_gather | solution.py:63
  265.1 6.3 copy.28
  271.4 12.7 %convolution_convert_fusion.1 = bf16[2,512,2,128]{3,1,2,0:T(8,128)(2,1)} fusion(bf16[2,128,8192,1]{2,1,0,3:T(8,128)(2,1)} %bitcast.70, bf16[2,512,8192]{2,1,0:T(8,128)(2,1)} %all-gather.8.cloned.1.call-done, f32[8192]{0:T(1024)S(1)} %copy-done.2, f32[2,512]{1,0:T(2,128)S(1)} %add_rsqrt_fusion), kind=kOutput, calls=%fused_computation.47 | convolution fusion | flops 4328783872 | bytes 21532672 | tf_op jit(solution)/shard_map/dot_general | solution.py:66
  285.2 131.2 %all-gather.14.cloned.1.call-done = bf16[8192,1024]{1,0:T(8,128)(2,1)} async-done(((bf16[1024,1024]{1,0:T(8,128)(2,1)}), bf16[8192,1024]{1,0:T(8,128)(2,1)}) %all-gather.14.cloned.1.call-update) | async-done | bytes 16777232 | tf_op jit(solution)/shard_map/all_gather | solution.py:61
  416.4 21.4 %copy.25 = bf16[1024,8192]{1,0:T(8,128)(2,1)} copy(bf16[1024,8192]{0,1:T(8,128)(2,1)} %bitcast.63) | data formatting | bytes 33554432 | tf_op jit(solution)/shard_map/dot_general | solution.py:66
  437.9 22.4 %fusion.27 = f32[2,512,8,128]{1,3,2,0:T(8,128)S(1)} fusion(bf16[8,128,8192,1]{2,1,0,3:T(8,128)(2,1)} %bitcast.64, bf16[2,512,8192]{2,1,0:T(8,128)(2,1)} %all-gather.8.cloned.1.call-done, f32[8192]{0:T(1024)S(1)} %copy-done.2, f32[2,512]{1,0:T(2,128)S(1)} %add_rsqrt_fusion), kind=kOutput, calls=%fused_computation.48 | convolution fusion | flops 17213423616 | bytes 37785600 | tf_op jit(solution)/shard_map/dot_general | solution.py:66
  469.9 6.4 copy.29
  476.3 33.8 %all-gather.18.cloned.1.call-done = bf16[2,4096,2,128]{3,1,2,0:T(8,128)(2,1)} async-done(((bf16[2,512,2,128]{3,1,2,0:T(8,128)(2,1)}), bf16[2,4096,2,128]{3,1,2,0:T(8,128)(2,1)}) %all-gather.18.cloned.1.call-update) | async-done | bytes 4194320 | tf_op jit(solution)/shard_map/all_gather | solution.py:81
  512.6 156.1 %while.19 = (s32[]{:T(128)}, f32[2,2,4,512]{3,2,1,0:T(4,128)S(1)}, f32[2,2,4,512]{3,2,1,0:T(4,128)S(1)}, f32[2,2,4,512,128]{4,3,2,1,0:T(8,128)}, s32[2,16]{1,0:T...) while((s32[]{:T(128)}, f32[2,2,4,512]{3,2,1,0:T(4,128)S(1)}, ...), condition=%wide.region_11.12_spmd, body=%wide.region_3.11_spmd.sunk | while | flops 2204700672 | bytes 64532936 | solution.py:117
  514.2 17.9 %conditional.2 = (f32[2,2,4,512]{3,2,1,0:T(4,128)S(1)}, f32[2,2,4,512]{3,2,1,0:T(4,128)S(1)}, f32[2,2,4,512,128]{4,3,2,1,0:T(8,128)}) conditional(s32[]{:T(128)} %convert_element_type.85, (s32[2,512]{1,0:T(2,128)S(1)}, s32[2,512]{1,0:T(2,128)S(1)}, s32[]{:T(128)}, bf16[2,4096,2,128]{3,1,2,0:T(8,128)(2,1)}, bf16[2,2,4,512,128]{4,3,2,1,0:T(8,128)(2,1)}, ...), branch_computations={%region_7.9_spmd, %region_10.10_spmd} | conditional | flops 2204647424 | bytes 64430148 | solution.py:113
  514.6 4.7 fusion
  519.3 4.1 fusion.2
  523.5 8.7 %multiply_add_fusion = f32[2,2,4,512,128]{4,3,2,1,0:T(8,128)} fusion(f32[2,2,4,512,128]{4,3,2,1,0:T(8,128)} %get-tuple-element.360, f32[2,2,4,512]{3,2,1,0:T(4,128)S(1)} %bitcast.76, f32[2,2,512,4,512]{4,2,3,1,0:T(8,128)S(1)} %get-tuple-element.437, f32[2,2,4,512]{3,2,1,0:T(4,128)S(1)} %max.5, pred[2,512,512]{1,2,0:T(8,128)(4,1)S(1)} %broadcast_compare_fusion, ...), kind=kOutput, calls=%fused_computation.7 | convolution fusion | flops 1096810496 | bytes 26279940 | tf_op jit(solution)/shard_map/while/body/eval_jaxpr/cond/branch_0_fun/shgqk,skhd->shgqd/dot_general | solution.py:105
  533.8 17.9 %conditional.2 = (f32[2,2,4,512]{3,2,1,0:T(4,128)S(1)}, f32[2,2,4,512]{3,2,1,0:T(4,128)S(1)}, f32[2,2,4,512,128]{4,3,2,1,0:T(8,128)}) conditional(s32[]{:T(128)} %convert_element_type.85, (s32[2,512]{1,0:T(2,128)S(1)}, s32[2,512]{1,0:T(2,128)S(1)}, s32[]{:T(128)}, bf16[2,4096,2,128]{3,1,2,0:T(8,128)(2,1)}, bf16[2,2,4,512,128]{4,3,2,1,0:T(8,128)(2,1)}, ...), branch_computations={%region_7.9_spmd, %region_10.10_spmd} | conditional | flops 2204647424 | bytes 64430148 | solution.py:113
  534.2 4.7 fusion
  538.9 4.1 fusion.2
  543.0 8.7 %multiply_add_fusion = f32[2,2,4,512,128]{4,3,2,1,0:T(8,128)} fusion(f32[2,2,4,512,128]{4,3,2,1,0:T(8,128)} %get-tuple-element.360, f32[2,2,4,512]{3,2,1,0:T(4,128)S(1)} %bitcast.76, f32[2,2,512,4,512]{4,2,3,1,0:T(8,128)S(1)} %get-tuple-element.437, f32[2,2,4,512]{3,2,1,0:T(4,128)S(1)} %max.5, pred[2,512,512]{1,2,0:T(8,128)(4,1)S(1)} %broadcast_compare_fusion, ...), kind=kOutput, calls=%fused_computation.7 | convolution fusion | flops 1096810496 | bytes 26279940 | tf_op jit(solution)/shard_map/while/body/eval_jaxpr/cond/branch_0_fun/shgqk,skhd->shgqd/dot_general | solution.py:105
  553.3 17.9 %conditional.2 = (f32[2,2,4,512]{3,2,1,0:T(4,128)S(1)}, f32[2,2,4,512]{3,2,1,0:T(4,128)S(1)}, f32[2,2,4,512,128]{4,3,2,1,0:T(8,128)}) conditional(s32[]{:T(128)} %convert_element_type.85, (s32[2,512]{1,0:T(2,128)S(1)}, s32[2,512]{1,0:T(2,128)S(1)}, s32[]{:T(128)}, bf16[2,4096,2,128]{3,1,2,0:T(8,128)(2,1)}, bf16[2,2,4,512,128]{4,3,2,1,0:T(8,128)(2,1)}, ...), branch_computations={%region_7.9_spmd, %region_10.10_spmd} | conditional | flops 2204647424 | bytes 64430148 | solution.py:113
  553.7 4.7 fusion
  558.4 4.1 fusion.2
  562.5 8.7 %multiply_add_fusion = f32[2,2,4,512,128]{4,3,2,1,0:T(8,128)} fusion(f32[2,2,4,512,128]{4,3,2,1,0:T(8,128)} %get-tuple-element.360, f32[2,2,4,512]{3,2,1,0:T(4,128)S(1)} %bitcast.76, f32[2,2,512,4,512]{4,2,3,1,0:T(8,128)S(1)} %get-tuple-element.437, f32[2,2,4,512]{3,2,1,0:T(4,128)S(1)} %max.5, pred[2,512,512]{1,2,0:T(8,128)(4,1)S(1)} %broadcast_compare_fusion, ...), kind=kOutput, calls=%fused_computation.7 | convolution fusion | flops 1096810496 | bytes 26279940 | tf_op jit(solution)/shard_map/while/body/eval_jaxpr/cond/branch_0_fun/shgqk,skhd->shgqd/dot_general | solution.py:105
  572.8 17.9 %conditional.2 = (f32[2,2,4,512]{3,2,1,0:T(4,128)S(1)}, f32[2,2,4,512]{3,2,1,0:T(4,128)S(1)}, f32[2,2,4,512,128]{4,3,2,1,0:T(8,128)}) conditional(s32[]{:T(128)} %convert_element_type.85, (s32[2,512]{1,0:T(2,128)S(1)}, s32[2,512]{1,0:T(2,128)S(1)}, s32[]{:T(128)}, bf16[2,4096,2,128]{3,1,2,0:T(8,128)(2,1)}, bf16[2,2,4,512,128]{4,3,2,1,0:T(8,128)(2,1)}, ...), branch_computations={%region_7.9_spmd, %region_10.10_spmd} | conditional | flops 2204647424 | bytes 64430148 | solution.py:113
  573.2 4.7 fusion
  577.9 4.1 fusion.2
  582.0 8.7 %multiply_add_fusion = f32[2,2,4,512,128]{4,3,2,1,0:T(8,128)} fusion(f32[2,2,4,512,128]{4,3,2,1,0:T(8,128)} %get-tuple-element.360, f32[2,2,4,512]{3,2,1,0:T(4,128)S(1)} %bitcast.76, f32[2,2,512,4,512]{4,2,3,1,0:T(8,128)S(1)} %get-tuple-element.437, f32[2,2,4,512]{3,2,1,0:T(4,128)S(1)} %max.5, pred[2,512,512]{1,2,0:T(8,128)(4,1)S(1)} %broadcast_compare_fusion, ...), kind=kOutput, calls=%fused_computation.7 | convolution fusion | flops 1096810496 | bytes 26279940 | tf_op jit(solution)/shard_map/while/body/eval_jaxpr/cond/branch_0_fun/shgqk,skhd->shgqd/dot_general | solution.py:105
  592.3 17.9 %conditional.2 = (f32[2,2,4,512]{3,2,1,0:T(4,128)S(1)}, f32[2,2,4,512]{3,2,1,0:T(4,128)S(1)}, f32[2,2,4,512,128]{4,3,2,1,0:T(8,128)}) conditional(s32[]{:T(128)} %convert_element_type.85, (s32[2,512]{1,0:T(2,128)S(1)}, s32[2,512]{1,0:T(2,128)S(1)}, s32[]{:T(128)}, bf16[2,4096,2,128]{3,1,2,0:T(8,128)(2,1)}, bf16[2,2,4,512,128]{4,3,2,1,0:T(8,128)(2,1)}, ...), branch_computations={%region_7.9_spmd, %region_10.10_spmd} | conditional | flops 2204647424 | bytes 64430148 | solution.py:113
  592.7 4.8 fusion
  597.5 4.1 fusion.2
  601.7 8.6 multiply_add_fusion
  611.9 17.8 %conditional.2 = (f32[2,2,4,512]{3,2,1,0:T(4,128)S(1)}, f32[2,2,4,512]{3,2,1,0:T(4,128)S(1)}, f32[2,2,4,512,128]{4,3,2,1,0:T(8,128)}) conditional(s32[]{:T(128)} %convert_element_type.85, (s32[2,512]{1,0:T(2,128)S(1)}, s32[2,512]{1,0:T(2,128)S(1)}, s32[]{:T(128)}, bf16[2,4096,2,128]{3,1,2,0:T(8,128)(2,1)}, bf16[2,2,4,512,128]{4,3,2,1,0:T(8,128)(2,1)}, ...), branch_computations={%region_7.9_spmd, %region_10.10_spmd} | conditional | flops 2204647424 | bytes 64430148 | solution.py:113
  612.3 4.7 fusion
  617.0 4.1 fusion.2
  621.1 8.6 multiply_add_fusion
  631.4 17.8 %conditional.2 = (f32[2,2,4,512]{3,2,1,0:T(4,128)S(1)}, f32[2,2,4,512]{3,2,1,0:T(4,128)S(1)}, f32[2,2,4,512,128]{4,3,2,1,0:T(8,128)}) conditional(s32[]{:T(128)} %convert_element_type.85, (s32[2,512]{1,0:T(2,128)S(1)}, s32[2,512]{1,0:T(2,128)S(1)}, s32[]{:T(128)}, bf16[2,4096,2,128]{3,1,2,0:T(8,128)(2,1)}, bf16[2,2,4,512,128]{4,3,2,1,0:T(8,128)(2,1)}, ...), branch_computations={%region_7.9_spmd, %region_10.10_spmd} | conditional | flops 2204647424 | bytes 64430148 | solution.py:113
  631.7 4.7 fusion
  636.5 4.1 fusion.2
  640.6 8.6 multiply_add_fusion
  650.8 17.9 %conditional.2 = (f32[2,2,4,512]{3,2,1,0:T(4,128)S(1)}, f32[2,2,4,512]{3,2,1,0:T(4,128)S(1)}, f32[2,2,4,512,128]{4,3,2,1,0:T(8,128)}) conditional(s32[]{:T(128)} %convert_element_type.85, (s32[2,512]{1,0:T(2,128)S(1)}, s32[2,512]{1,0:T(2,128)S(1)}, s32[]{:T(128)}, bf16[2,4096,2,128]{3,1,2,0:T(8,128)(2,1)}, bf16[2,2,4,512,128]{4,3,2,1,0:T(8,128)(2,1)}, ...), branch_computations={%region_7.9_spmd, %region_10.10_spmd} | conditional | flops 2204647424 | bytes 64430148 | solution.py:113
  651.2 4.7 fusion
  655.9 4.1 fusion.2
  660.0 8.7 %multiply_add_fusion = f32[2,2,4,512,128]{4,3,2,1,0:T(8,128)} fusion(f32[2,2,4,512,128]{4,3,2,1,0:T(8,128)} %get-tuple-element.360, f32[2,2,4,512]{3,2,1,0:T(4,128)S(1)} %bitcast.76, f32[2,2,512,4,512]{4,2,3,1,0:T(8,128)S(1)} %get-tuple-element.437, f32[2,2,4,512]{3,2,1,0:T(4,128)S(1)} %max.5, pred[2,512,512]{1,2,0:T(8,128)(4,1)S(1)} %broadcast_compare_fusion, ...), kind=kOutput, calls=%fused_computation.7 | convolution fusion | flops 1096810496 | bytes 26279940 | tf_op jit(solution)/shard_map/while/body/eval_jaxpr/cond/branch_0_fun/shgqk,skhd->shgqd/dot_general | solution.py:105
  676.1 26.4 %convolution_convert_fusion = bf16[1024,8192]{1,0:T(8,128)(2,1)} fusion(bf16[1024,1024]{1,0:T(8,128)(2,1)} %reshape.213, bf16[1024,8192]{1,0:T(8,128)(2,1)} %all-gather.20.cloned.1.call-done), kind=kOutput, calls=%fused_computation.41 | convolution fusion | flops 17188257792 | bytes 35651584 | tf_op jit(solution)/shard_map/dot_general | solution.py:120
  702.6 152.7 %reduce-scatter.2.cloned.1.call-done = bf16[1024,2048]{1,0:T(8,128)(2,1)} async-done(((bf16[1024,8192]{1,0:T(8,128)(2,1)}), bf16[1024,2048]{1,0:T(8,128)(2,1)}) %reduce-scatter.2.cloned.1.call-update) | async-done | bytes 4194320 | tf_op jit(solution)/shard_map/reduce_scatter | solution.py:125
  (116 shorter events, 36.3 us)
Async XLA Ops:
  6.5 2.9 copy-start.1
  6.5 52.0 %all-gather.10.cloned.1.call-start = ((), (), s32[]{:S(2)}) async-start(), calls=%async_computation.2 | async-start | bytes 4718592 | tf_op jit(solution)/shard_map/all_gather | solution.py:62
  7.3 209.3 %all-gather.8.cloned.1.call-start = ((), (), s32[]{:S(2)}) async-start(), calls=%async_computation.1 | async-start | bytes 20971520 | tf_op jit(solution)/shard_map/all_gather | solution.py:50
  8.0 257.0 %all-gather.16.cloned.1.call-start = ((), (), s32[]{:S(2)}) async-start(), calls=%async_computation.5 | async-start | bytes 4718592 | tf_op jit(solution)/shard_map/all_gather | solution.py:63
  8.7 407.7 %all-gather.14.cloned.1.call-start = ((), (), s32[]{:S(2)}) async-start(), calls=%async_computation.4 | async-start | bytes 18874368 | tf_op jit(solution)/shard_map/all_gather | solution.py:61
  9.3 460.5 %all-gather.12.cloned.1.call-start = ((), (), s32[]{:S(2)}) async-start(), calls=%async_computation.3 | async-start | bytes 4718592 | tf_op jit(solution)/shard_map/all_gather | solution.py:80
  64.9 159.1 %copy-start.2 = (f32[8192]{0:T(1024)S(1)}, f32[8192]{0:T(1024)}, u32[]{:S(2)}) copy-start(f32[8192]{0:T(1024)} %param.12) | copy-start | bytes 98308
  216.5 7.5 copy-start
  234.1 276.0 %all-gather.18.cloned.1.call-start = ((), (), s32[]{:S(2)}) async-start(), calls=%async_computation.6 | async-start | bytes 4718592 | tf_op jit(solution)/shard_map/all_gather | solution.py:81
  284.1 392.1 %all-gather.20.cloned.1.call-start = ((), (), s32[]{:S(2)}) async-start(), calls=%async_computation.7 | async-start | bytes 18874368 | tf_op jit(solution)/shard_map/all_gather | solution.py:122
  284.8 570.4 %reduce-scatter.2.cloned.1.call-start = ((), (), s32[]{:S(2)}) async-start(), calls=%async_computation.8 | async-start | bytes 20971520 | tf_op jit(solution)/shard_map/reduce_scatter | solution.py:125
Sparse Core Ops, SparseCore 0:
  8.9 49.5 all-gather.9
  60.4 156.0 all-gather.7
  218.1 46.8 all-gather.15
  266.5 149.8 all-gather.13
  417.9 45.0 all-gather.11
  464.4 45.6 all-gather.17
  511.7 149.8 all-gather.19
  702.7 152.5 reduce-scatter.1
where the time goes:
time: 864 us; the launch traced here: 862 us
  waiting for transfers between devices  552 us (64%)
  matrix products  177 us (20%)
  other arithmetic  62 us (7%)
  local copies, waits for them, and re-layouts  51.1 us (6%)
  between operations  13.6 us (2%)
    reduce_scatter x1, waiting for transfers between devices, per_device(): lax.psum_scatter(terms.astype(jnp.bfloat16), 'tp', scatter_dimension=1, t...  153 us
    all_gather x1, waiting for transfers between devices, per_device(): whole = lax.all_gather(tokens, 'tp', axis=2, tiled=True)  152 us
    all_gather x1, waiting for transfers between devices, per_device(): lax.all_gather(w_query, 'ctx', axis=0, tiled=True)  131 us
    dot_general x8, matrix products, update(): jnp.einsum('shgqk,skhd->shgqd', weights.astype(jnp.bfloat16), value_block...  69.1 us
    all_gather x1, waiting for transfers between devices, per_device(): lax.all_gather(w_key, 'ctx', axis=0, tiled=True)  48 us
    dot_general x3, matrix products, per_device(): jnp.dot(normed, piece, preferred_element_type=jnp.float32)  44.1 us
    dot_general x8, matrix products, update(): jnp.einsum('shgqd,skhd->shgqk', query, key_block, preferred_element_type=...  37.6 us
    dot_general x3, local copies, waits for them, and re-layouts, per_device(): jnp.dot(normed, piece, preferred_element_type=jnp.float32)  34.1 us
  transfers between devices with their start and end apart: 8, of which 6 were waited for; matrix products, arithmetic and copies ran while one was open for 31% of the time, Pallas kernels for 0%

commit v1 on v0

--- a/solution.py
+++ b/solution.py
@@ -47,7 +47,8 @@
     total_rows = sequence_batch * rows_dev
     factor = 1.0 / math.sqrt(head_size)
     rank = lax.axis_index("ctx")
-    whole = lax.all_gather(tokens, "tp", axis=2, tiled=True)
+    shards = lax.all_gather(tokens, "tp", axis=0, tiled=False)
+    whole = jnp.concatenate(shards, axis=2)
     normed = normalize(whole.reshape(total_rows, whole.shape[2]), norm_gain)
     query_pos = positions_of(span_order, rank * rows_dev, rows_dev, block_rows)
     latest = jnp.max(query_pos, axis=1)

time: 864 us -> 865 us (level)
  waiting for transfers between devices: 552 us -> 476 us
  local copies, waits for them, and re-layouts: 51.1 us -> 123 us
    convert_element_type x0 -> x2, local copies, waits for them, and re-layouts: none -> 68 us  [normalize(): return (wide * factor * norm_gain).astype(jnp.bfloat16)]
    all_gather x1, waiting for transfers between devices: 131 us -> 86.5 us  [per_device(): lax.all_gather(w_query, 'ctx', axis=0, tiled=True)]
    all_gather x1, waiting for transfers between devices: 30.9 us -> 0.02 us  [per_device(): lax.all_gather(value_weight, 'ctx', axis=0, tiled=True)]
  transfers between devices with their start and end apart: 8 -> 8, of which waited for: 6 -> 5; matrix products, arithmetic and copies ran while one was open for 31% -> 39% of each run, Pallas kernels for 0% -> 0%
where the time goes in v1:
time: 865 us; the launch traced here: 862 us
  waiting for transfers between devices  476 us (55%)
  matrix products  175 us (20%)
  local copies, waits for them, and re-layouts  123 us (14%)
  other arithmetic  67.6 us (8%)
  between operations  13.6 us (2%)
    reduce_scatter x1, waiting for transfers between devices, per_device(): lax.psum_scatter(terms.astype(jnp.bfloat16), 'tp', scatter_dimension=1, t...  153 us
    all_gather x1, waiting for transfers between devices, per_device(): shards = lax.all_gather(tokens, 'tp', axis=0, tiled=False)  152 us
    all_gather x1, waiting for transfers between devices, per_device(): lax.all_gather(w_query, 'ctx', axis=0, tiled=True)  86.5 us
    dot_general x8, matrix products, update(): jnp.einsum('shgqk,skhd->shgqd', weights.astype(jnp.bfloat16), value_block...  69.1 us
    convert_element_type x2, local copies, waits for them, and re-layouts, normalize(): return (wide * factor * norm_gain).astype(jnp.bfloat16)  68 us
    all_gather x1, waiting for transfers between devices, per_device(): lax.all_gather(w_key, 'ctx', axis=0, tiled=True)  48 us
    dot_general x3, matrix products, per_device(): jnp.dot(normed, piece, preferred_element_type=jnp.float32)  41.7 us
    dot_general x8, matrix products, update(): jnp.einsum('shgqd,skhd->shgqk', query, key_block, preferred_element_type=...  37.6 us
  transfers between devices with their start and end apart: 8, of which 5 were waited for; matrix products, arithmetic and copies ran while one was open for 39% of the time, Pallas kernels for 0%

profile of v1, /device:TPU:0, one launch (start us, length us, event | category | flops | bytes accessed | tf_op | source)
XLA Modules:
  0.0 862.1 jit_solution(6097449967442795863)
XLA Ops:
  10.6 48.0 %all-gather.9.cloned.1.call-done = bf16[8192,256]{1,0:T(8,128)(2,1)} async-done(((bf16[1024,256]{1,0:T(8,128)(2,1)}), bf16[8192,256]{1,0:T(8,128)(2,1)}) %all-gather.9.cloned.1.call-update) | async-done | bytes 4194320 | tf_op jit(solution)/shard_map/all_gather | solution.py:63
  58.6 6.3 copy.36
  64.9 151.6 %all-gather.21.cloned.1.call-done = bf16[8,512,2048]{2,1,0:T(8,128)(2,1)} async-done(((bf16[2,512,2048]{2,1,0:T(8,128)(2,1)}), bf16[8,512,2048]{2,1,0:T(8,128)(2,1)}) %all-gather.21.cloned.1.call-update) | async-done | bytes 16777232 | tf_op jit(solution)/shard_map/all_gather | solution.py:50
  216.5 7.5 fusion.21
  227.9 5.6 fusion.24
  233.5 40.2 %copy.35 = bf16[2,512,4,2048]{3,2,1,0:T(4,128)(2,1)} copy(bf16[2,512,4,2048]{3,1,0,2:T(8,128)(2,1)S(1)} %fusion.24) | data formatting | bytes 33554432 | tf_op jit(solution)/shard_map/convert_element_type | solution.py:16
  273.7 27.9 %reshape.244 = bf16[2,512,8192,1]{2,1,0,3:T(8,128)(2,1)} reshape(bf16[2,512,4,2048]{3,2,1,0:T(4,128)(2,1)} %copy.35) | data formatting | bytes 33554432 | tf_op jit(solution)/shard_map/convert_element_type | solution.py:16
  301.5 9.7 %fusion.29 = f32[2,512,2,128]{1,3,2,0:T(8,128)S(1)} fusion(bf16[2,128,8192,1]{2,1,0,3:T(8,128)(2,1)} %bitcast.77, bf16[2,512,8192,1]{2,1,0,3:T(8,128)(2,1)} %reshape.244), kind=kOutput, calls=%fused_computation.45 | convolution fusion | flops 4294967296 | bytes 22020096 | tf_op jit(solution)/shard_map/dot_general | solution.py:67
  312.4 6.4 copy.40
  318.7 10.1 %fusion.32 = bf16[2,512,2,128]{3,1,2,0:T(8,128)(2,1)} fusion(bf16[2,128,8192,1]{2,1,0,3:T(8,128)(2,1)} %bitcast.78, bf16[2,512,8192,1]{2,1,0,3:T(8,128)(2,1)} %reshape.244), kind=kOutput, calls=%fused_computation.53 | convolution fusion | flops 4295229440 | bytes 21495808 | tf_op jit(solution)/shard_map/dot_general | solution.py:67
  329.9 86.5 %all-gather.13.cloned.1.call-done = bf16[8192,1024]{1,0:T(8,128)(2,1)} async-done(((bf16[1024,1024]{1,0:T(8,128)(2,1)}), bf16[8192,1024]{1,0:T(8,128)(2,1)}) %all-gather.13.cloned.1.call-update) | async-done | bytes 16777232 | tf_op jit(solution)/shard_map/all_gather | solution.py:62
  416.4 21.4 %copy.37 = bf16[1024,8192]{1,0:T(8,128)(2,1)} copy(bf16[1024,8192]{0,1:T(8,128)(2,1)} %bitcast.71) | data formatting | bytes 33554432 | tf_op jit(solution)/shard_map/dot_general | solution.py:67
  437.8 22.0 %fusion.27 = f32[2,512,8,128]{1,3,2,0:T(8,128)S(1)} fusion(bf16[8,128,8192,1]{2,1,0,3:T(8,128)(2,1)} %bitcast.72, bf16[2,512,8192,1]{2,1,0,3:T(8,128)(2,1)} %reshape.244), kind=kOutput, calls=%fused_computation.43 | convolution fusion | flops 17179869184 | bytes 37748736 | tf_op jit(solution)/shard_map/dot_general | solution.py:67
  469.4 6.4 copy.41
  475.8 34.3 %all-gather.17.cloned.1.call-done = bf16[2,4096,2,128]{3,1,2,0:T(8,128)(2,1)} async-done(((bf16[2,512,2,128]{3,1,2,0:T(8,128)(2,1)}), bf16[2,4096,2,128]{3,1,2,0:T(8,128)(2,1)}) %all-gather.17.cloned.1.call-update) | async-done | bytes 4194320 | tf_op jit(solution)/shard_map/all_gather | solution.py:82
  512.6 156.1 %while.19 = (s32[]{:T(128)}, f32[2,2,4,512]{3,2,1,0:T(4,128)S(1)}, f32[2,2,4,512]{3,2,1,0:T(4,128)S(1)}, f32[2,2,4,512,128]{4,3,2,1,0:T(8,128)}, s32[2,16]{1,0:T...) while((s32[]{:T(128)}, f32[2,2,4,512]{3,2,1,0:T(4,128)S(1)}, ...), condition=%wide.region_11.12_spmd, body=%wide.region_3.11_spmd.sunk | while | flops 2204700672 | bytes 64532936 | solution.py:118
  514.2 17.9 %conditional.2 = (f32[2,2,4,512]{3,2,1,0:T(4,128)S(1)}, f32[2,2,4,512]{3,2,1,0:T(4,128)S(1)}, f32[2,2,4,512,128]{4,3,2,1,0:T(8,128)}) conditional(s32[]{:T(128)} %convert_element_type.96, (s32[2,512]{1,0:T(2,128)S(1)}, s32[2,512]{1,0:T(2,128)S(1)}, s32[]{:T(128)}, bf16[2,4096,2,128]{3,1,2,0:T(8,128)(2,1)}, bf16[2,2,4,512,128]{4,3,2,1,0:T(8,128)(2,1)}, ...), branch_computations={%region_7.9_spmd, %region_10.10_spmd} | conditional | flops 2204647424 | bytes 64430148 | solution.py:114
  514.6 4.7 fusion
  519.3 4.1 fusion.2
  523.4 8.7 %multiply_add_fusion = f32[2,2,4,512,128]{4,3,2,1,0:T(8,128)} fusion(f32[2,2,4,512,128]{4,3,2,1,0:T(8,128)} %get-tuple-element.360, f32[2,2,4,512]{3,2,1,0:T(4,128)S(1)} %bitcast.84, f32[2,2,512,4,512]{4,2,3,1,0:T(8,128)S(1)} %get-tuple-element.447, f32[2,2,4,512]{3,2,1,0:T(4,128)S(1)} %max.5, pred[2,512,512]{1,2,0:T(8,128)(4,1)S(1)} %broadcast_compare_fusion, ...), kind=kOutput, calls=%fused_computation.7 | convolution fusion | flops 1096810496 | bytes 26279940 | tf_op jit(solution)/shard_map/while/body/eval_jaxpr/cond/branch_0_fun/shgqk,skhd->shgqd/dot_general | solution.py:106
  533.8 17.9 %conditional.2 = (f32[2,2,4,512]{3,2,1,0:T(4,128)S(1)}, f32[2,2,4,512]{3,2,1,0:T(4,128)S(1)}, f32[2,2,4,512,128]{4,3,2,1,0:T(8,128)}) conditional(s32[]{:T(128)} %convert_element_type.96, (s32[2,512]{1,0:T(2,128)S(1)}, s32[2,512]{1,0:T(2,128)S(1)}, s32[]{:T(128)}, bf16[2,4096,2,128]{3,1,2,0:T(8,128)(2,1)}, bf16[2,2,4,512,128]{4,3,2,1,0:T(8,128)(2,1)}, ...), branch_computations={%region_7.9_spmd, %region_10.10_spmd} | conditional | flops 2204647424 | bytes 64430148 | solution.py:114
  534.1 4.7 fusion
  538.9 4.1 fusion.2
  543.0 8.7 %multiply_add_fusion = f32[2,2,4,512,128]{4,3,2,1,0:T(8,128)} fusion(f32[2,2,4,512,128]{4,3,2,1,0:T(8,128)} %get-tuple-element.360, f32[2,2,4,512]{3,2,1,0:T(4,128)S(1)} %bitcast.84, f32[2,2,512,4,512]{4,2,3,1,0:T(8,128)S(1)} %get-tuple-element.447, f32[2,2,4,512]{3,2,1,0:T(4,128)S(1)} %max.5, pred[2,512,512]{1,2,0:T(8,128)(4,1)S(1)} %broadcast_compare_fusion, ...), kind=kOutput, calls=%fused_computation.7 | convolution fusion | flops 1096810496 | bytes 26279940 | tf_op jit(solution)/shard_map/while/body/eval_jaxpr/cond/branch_0_fun/shgqk,skhd->shgqd/dot_general | solution.py:106
  553.3 17.9 %conditional.2 = (f32[2,2,4,512]{3,2,1,0:T(4,128)S(1)}, f32[2,2,4,512]{3,2,1,0:T(4,128)S(1)}, f32[2,2,4,512,128]{4,3,2,1,0:T(8,128)}) conditional(s32[]{:T(128)} %convert_element_type.96, (s32[2,512]{1,0:T(2,128)S(1)}, s32[2,512]{1,0:T(2,128)S(1)}, s32[]{:T(128)}, bf16[2,4096,2,128]{3,1,2,0:T(8,128)(2,1)}, bf16[2,2,4,512,128]{4,3,2,1,0:T(8,128)(2,1)}, ...), branch_computations={%region_7.9_spmd, %region_10.10_spmd} | conditional | flops 2204647424 | bytes 64430148 | solution.py:114
  553.7 4.7 fusion
  558.4 4.1 fusion.2
  562.5 8.7 %multiply_add_fusion = f32[2,2,4,512,128]{4,3,2,1,0:T(8,128)} fusion(f32[2,2,4,512,128]{4,3,2,1,0:T(8,128)} %get-tuple-element.360, f32[2,2,4,512]{3,2,1,0:T(4,128)S(1)} %bitcast.84, f32[2,2,512,4,512]{4,2,3,1,0:T(8,128)S(1)} %get-tuple-element.447, f32[2,2,4,512]{3,2,1,0:T(4,128)S(1)} %max.5, pred[2,512,512]{1,2,0:T(8,128)(4,1)S(1)} %broadcast_compare_fusion, ...), kind=kOutput, calls=%fused_computation.7 | convolution fusion | flops 1096810496 | bytes 26279940 | tf_op jit(solution)/shard_map/while/body/eval_jaxpr/cond/branch_0_fun/shgqk,skhd->shgqd/dot_general | solution.py:106
  572.8 17.9 %conditional.2 = (f32[2,2,4,512]{3,2,1,0:T(4,128)S(1)}, f32[2,2,4,512]{3,2,1,0:T(4,128)S(1)}, f32[2,2,4,512,128]{4,3,2,1,0:T(8,128)}) conditional(s32[]{:T(128)} %convert_element_type.96, (s32[2,512]{1,0:T(2,128)S(1)}, s32[2,512]{1,0:T(2,128)S(1)}, s32[]{:T(128)}, bf16[2,4096,2,128]{3,1,2,0:T(8,128)(2,1)}, bf16[2,2,4,512,128]{4,3,2,1,0:T(8,128)(2,1)}, ...), branch_computations={%region_7.9_spmd, %region_10.10_spmd} | conditional | flops 2204647424 | bytes 64430148 | solution.py:114
  573.2 4.7 fusion
  577.9 4.1 fusion.2
  582.0 8.7 %multiply_add_fusion = f32[2,2,4,512,128]{4,3,2,1,0:T(8,128)} fusion(f32[2,2,4,512,128]{4,3,2,1,0:T(8,128)} %get-tuple-element.360, f32[2,2,4,512]{3,2,1,0:T(4,128)S(1)} %bitcast.84, f32[2,2,512,4,512]{4,2,3,1,0:T(8,128)S(1)} %get-tuple-element.447, f32[2,2,4,512]{3,2,1,0:T(4,128)S(1)} %max.5, pred[2,512,512]{1,2,0:T(8,128)(4,1)S(1)} %broadcast_compare_fusion, ...), kind=kOutput, calls=%fused_computation.7 | convolution fusion | flops 1096810496 | bytes 26279940 | tf_op jit(solution)/shard_map/while/body/eval_jaxpr/cond/branch_0_fun/shgqk,skhd->shgqd/dot_general | solution.py:106
  592.3 17.9 %conditional.2 = (f32[2,2,4,512]{3,2,1,0:T(4,128)S(1)}, f32[2,2,4,512]{3,2,1,0:T(4,128)S(1)}, f32[2,2,4,512,128]{4,3,2,1,0:T(8,128)}) conditional(s32[]{:T(128)} %convert_element_type.96, (s32[2,512]{1,0:T(2,128)S(1)}, s32[2,512]{1,0:T(2,128)S(1)}, s32[]{:T(128)}, bf16[2,4096,2,128]{3,1,2,0:T(8,128)(2,1)}, bf16[2,2,4,512,128]{4,3,2,1,0:T(8,128)(2,1)}, ...), branch_computations={%region_7.9_spmd, %region_10.10_spmd} | conditional | flops 2204647424 | bytes 64430148 | solution.py:114
  592.7 4.8 fusion
  597.5 4.1 fusion.2
  601.6 8.6 multiply_add_fusion
  611.9 17.8 %conditional.2 = (f32[2,2,4,512]{3,2,1,0:T(4,128)S(1)}, f32[2,2,4,512]{3,2,1,0:T(4,128)S(1)}, f32[2,2,4,512,128]{4,3,2,1,0:T(8,128)}) conditional(s32[]{:T(128)} %convert_element_type.96, (s32[2,512]{1,0:T(2,128)S(1)}, s32[2,512]{1,0:T(2,128)S(1)}, s32[]{:T(128)}, bf16[2,4096,2,128]{3,1,2,0:T(8,128)(2,1)}, bf16[2,2,4,512,128]{4,3,2,1,0:T(8,128)(2,1)}, ...), branch_computations={%region_7.9_spmd, %region_10.10_spmd} | conditional | flops 2204647424 | bytes 64430148 | solution.py:114
  612.3 4.7 fusion
  617.0 4.1 fusion.2
  621.1 8.6 multiply_add_fusion
  631.3 17.8 %conditional.2 = (f32[2,2,4,512]{3,2,1,0:T(4,128)S(1)}, f32[2,2,4,512]{3,2,1,0:T(4,128)S(1)}, f32[2,2,4,512,128]{4,3,2,1,0:T(8,128)}) conditional(s32[]{:T(128)} %convert_element_type.96, (s32[2,512]{1,0:T(2,128)S(1)}, s32[2,512]{1,0:T(2,128)S(1)}, s32[]{:T(128)}, bf16[2,4096,2,128]{3,1,2,0:T(8,128)(2,1)}, bf16[2,2,4,512,128]{4,3,2,1,0:T(8,128)(2,1)}, ...), branch_computations={%region_7.9_spmd, %region_10.10_spmd} | conditional | flops 2204647424 | bytes 64430148 | solution.py:114
  631.7 4.7 fusion
  640.6 8.6 multiply_add_fusion
  650.8 17.9 %conditional.2 = (f32[2,2,4,512]{3,2,1,0:T(4,128)S(1)}, f32[2,2,4,512]{3,2,1,0:T(4,128)S(1)}, f32[2,2,4,512,128]{4,3,2,1,0:T(8,128)}) conditional(s32[]{:T(128)} %convert_element_type.96, (s32[2,512]{1,0:T(2,128)S(1)}, s32[2,512]{1,0:T(2,128)S(1)}, s32[]{:T(128)}, bf16[2,4096,2,128]{3,1,2,0:T(8,128)(2,1)}, bf16[2,2,4,512,128]{4,3,2,1,0:T(8,128)(2,1)}, ...), branch_computations={%region_7.9_spmd, %region_10.10_spmd} | conditional | flops 2204647424 | bytes 64430148 | solution.py:114
  651.2 4.7 fusion
  660.0 8.7 %multiply_add_fusion = f32[2,2,4,512,128]{4,3,2,1,0:T(8,128)} fusion(f32[2,2,4,512,128]{4,3,2,1,0:T(8,128)} %get-tuple-element.360, f32[2,2,4,512]{3,2,1,0:T(4,128)S(1)} %bitcast.84, f32[2,2,512,4,512]{4,2,3,1,0:T(8,128)S(1)} %get-tuple-element.447, f32[2,2,4,512]{3,2,1,0:T(4,128)S(1)} %max.5, pred[2,512,512]{1,2,0:T(8,128)(4,1)S(1)} %broadcast_compare_fusion, ...), kind=kOutput, calls=%fused_computation.7 | convolution fusion | flops 1096810496 | bytes 26279940 | tf_op jit(solution)/shard_map/while/body/eval_jaxpr/cond/branch_0_fun/shgqk,skhd->shgqd/dot_general | solution.py:106
  676.1 26.4 %convolution_convert_fusion = bf16[1024,8192]{1,0:T(8,128)(2,1)} fusion(bf16[1024,1024]{1,0:T(8,128)(2,1)} %reshape.238, bf16[1024,8192]{1,0:T(8,128)(2,1)} %all-gather.19.cloned.1.call-done), kind=kOutput, calls=%fused_computation.47 | convolution fusion | flops 17188257792 | bytes 35651584 | tf_op jit(solution)/shard_map/dot_general | solution.py:121
  702.5 152.7 %reduce-scatter.2.cloned.1.call-done = bf16[1024,2048]{1,0:T(8,128)(2,1)} async-done(((bf16[1024,8192]{1,0:T(8,128)(2,1)}), bf16[1024,2048]{1,0:T(8,128)(2,1)}) %reduce-scatter.2.cloned.1.call-update) | async-done | bytes 4194320 | tf_op jit(solution)/shard_map/reduce_scatter | solution.py:126
  (120 shorter events, 48.4 us)
Async XLA Ops:
  6.5 2.8 copy-start.2
  6.5 2.9 copy-start.1
  6.5 52.0 %all-gather.9.cloned.1.call-start = ((), (), s32[]{:S(2)}) async-start(), calls=%async_computation.1 | async-start | bytes 4718592 | tf_op jit(solution)/shard_map/all_gather | solution.py:63
  7.3 209.3 %all-gather.21.cloned.1.call-start = ((), (), s32[]{:S(2)}) async-start(), calls=%async_computation.8 | async-start | bytes 20971520 | tf_op jit(solution)/shard_map/all_gather | solution.py:50
  8.0 304.3 %all-gather.15.cloned.1.call-start = ((), (), s32[]{:S(2)}) async-start(), calls=%async_computation.4 | async-start | bytes 4718592 | tf_op jit(solution)/shard_map/all_gather | solution.py:64
  8.7 407.7 %all-gather.13.cloned.1.call-start = ((), (), s32[]{:S(2)}) async-start(), calls=%async_computation.3 | async-start | bytes 18874368 | tf_op jit(solution)/shard_map/all_gather | solution.py:62
  9.3 460.1 %all-gather.11.cloned.1.call-start = ((), (), s32[]{:S(2)}) async-start(), calls=%async_computation.2 | async-start | bytes 4718592 | tf_op jit(solution)/shard_map/all_gather | solution.py:81
  216.5 11.4 %copy-start = (bf16[8,512,2048]{2,1,0:T(8,128)(2,1)S(1)}, bf16[8,512,2048]{2,1,0:T(8,128)(2,1)}, u32[]{:S(2)}) copy-start(bf16[8,512,2048]{2,1,0:T(8,128)(2,1)} %all-gather.21.cloned.1.call-done) | copy-start | bytes 50331652
  312.3 197.8 %all-gather.17.cloned.1.call-start = ((), (), s32[]{:S(2)}) async-start(), calls=%async_computation.5 | async-start | bytes 4718592 | tf_op jit(solution)/shard_map/all_gather | solution.py:82
  328.8 347.3 %all-gather.19.cloned.1.call-start = ((), (), s32[]{:S(2)}) async-start(), calls=%async_computation.6 | async-start | bytes 18874368 | tf_op jit(solution)/shard_map/all_gather | solution.py:123
  329.6 525.6 %reduce-scatter.2.cloned.1.call-start = ((), (), s32[]{:S(2)}) async-start(), calls=%async_computation.7 | async-start | bytes 20971520 | tf_op jit(solution)/shard_map/reduce_scatter | solution.py:126
Sparse Core Ops, SparseCore 0:
  8.9 49.5 all-gather.8
  60.4 156.0 all-gather.20
  218.1 46.8 all-gather.14
  266.5 149.8 all-gather.12
  417.9 45.0 all-gather.10
  464.4 45.6 all-gather.16
  511.7 149.8 all-gather.18
  702.7 152.5 reduce-scatter.1
